TPU v7x, 32 devices: a whole 2x2x4 slice. The times are simulated.
32 devices in a mesh: dp: 8 (over y, x, core), tensor: 4 (over z).
Axes of the slice: x: 2, y: 2, z: 4, core: 2. Of those that a mesh axis runs over, the one named last changes fastest.
Arguments:
- grad_out: bfloat16 [2048, 4096], P('dp'), may hold values from -6 to 6
- down_weight: bfloat16 [14336, 4096], P('tensor'), may hold values from -0.046875 to 0.046875
- gate_pre: bfloat16 [2048, 14336], P('dp', 'tensor'), may hold values from -8 to 8
- up_pre: bfloat16 [2048, 14336], P('dp', 'tensor'), may hold values from -6 to 6
Outputs:
- factor: float32 [14336, 14336], P('dp', 'tensor')
- grad_up: bfloat16 [2048, 14336], P('dp', 'tensor')
All inputs are finite; a program needn't handle non-finite values.
Results may differ from a plain program's by a relative error of at most 0.0046.
Values may be sent and summed in bfloat16 or wider, within the bound.
A program may use at most 128 MiB of HBM per device.

v0:
```python
import jax
import jax.numpy as jnp
from jax import lax
from jax.sharding import PartitionSpec as P


def local(grad_out, down_weight, gate_pre, up_pre):
    hidden_grad = lax.dot_general(
        grad_out, down_weight, (((1,), (1,)), ((), ())), preferred_element_type=jnp.float32
    )
    gate_value = gate_pre.astype(jnp.float32)
    sigmoid_gate = jax.nn.sigmoid(gate_value)
    silu_slope = sigmoid_gate * (1.0 + gate_value * (1.0 - sigmoid_gate))
    grad_gate = (hidden_grad * up_pre.astype(jnp.float32) * silu_slope).astype(jnp.bfloat16)
    grad_up = (hidden_grad * gate_value * sigmoid_gate).astype(jnp.bfloat16)
    replicas = lax.axis_size("dp")
    token_total = grad_gate.shape[0] * replicas
    all_columns_grad = lax.all_gather(grad_gate, "tensor", axis=1, tiled=True)
    row_block = lax.all_to_all(all_columns_grad, "dp", split_axis=1, concat_axis=0, tiled=True)
    factor_tile = lax.dot_general(
        row_block,
        lax.all_gather(grad_gate, "dp", axis=0, tiled=True),
        (((0,), (0,)), ((), ())),
        preferred_element_type=jnp.float32,
    )
    factor = factor_tile / jnp.float32(token_total)
    return (factor, grad_up)


def solution(mesh):
    placed = (P("dp", None), P("tensor", None), P("dp", "tensor"), P("dp", "tensor"))
    return jax.shard_map(
        local,
        mesh=mesh,
        in_specs=placed,
        out_specs=(P("dp", "tensor"), P("dp", "tensor")),
        check_vma=False,
    )
```

profile of v0, /device:TPU:0, one launch (start us, length us, event | category | flops | bytes accessed | tf_op | source)
XLA Modules:
  0.0 351.9 jit_solution(13841127326262000508)
XLA Ops:
  7.2 0.0 copy-start
  7.2 0.0 all-gather.3.cloned.1.call-start
  7.2 1.5 copy-done
  8.8 16.8 %fusion.8 = (bf16[256,3584]{1,0:T(8,128)(2,1)}, bf16[256,3584]{1,0:T(8,128)(2,1)}) fusion(bf16[256,3584]{1,0:T(8,128)(2,1)} %param.6, bf16[256,3584]{1,0:T(8,128)(2,1)} %param.7, bf16[256,4096]{1,0:T(8,128)(2,1)S(1)} %copy-done, bf16[3584,4096]{1,0:T(8,128)(2,1)} %param.5), kind=kOutput, calls=%fused_computation.13 | convolution fusion | flops 7529955328 | bytes 38797312 | tf_op jit(solution)/shard_map/dot_general | solution.py:8
  25.6 0.0 all-gather.3.cloned.1.call-update
  25.6 0.0 all-gather.5.cloned.1.call-start
  25.7 0.7 all-gather.5.cloned.1.call-update
  26.4 134.6 %all-gather.3.cloned.1.call-done = bf16[256,14336]{1,0:T(8,128)(2,1)} async-done(((bf16[256,3584]{1,0:T(8,128)(2,1)}), bf16[256,14336]{1,0:T(8,128)(2,1)}) %all-gather.3.cloned.1.call-update) | async-done | bytes 7340048 | tf_op jit(solution)/shard_map/all_gather | solution.py:18
  161.0 3.6 %copy.9 = bf16[32,8,8,1792]{3,2,0,1:T(8,128)(2,1)S(1)} copy(bf16[32,8,8,1792]{3,2,1,0:T(8,128)(2,1)} %bitcast.12) | data formatting | bytes 14680064 | tf_op jit(solution)/shard_map/all_to_all | solution.py:19
  164.5 135.2 %all_to_all.19 = bf16[256,8,1792]{2,0,1:T(8,128)(2,1)} all-to-all(bf16[256,8,1792]{2,0,1:T(8,128)(2,1)S(1)} %bitcast.11), channel_id=1, replica_groups=mesh['dp'=8,'tensor'=4] {'dp'}, dimensions={1} | all-to-all | bytes 14680064 | tf_op jit(solution)/shard_map/all_to_all | solution.py:19
  299.8 11.4 %all-gather.5.cloned.1.call-done = bf16[2048,3584]{1,0:T(8,128)(2,1)} async-done(((bf16[256,3584]{1,0:T(8,128)(2,1)}), bf16[2048,3584]{1,0:T(8,128)(2,1)}) %all-gather.5.cloned.1.call-update) | async-done | bytes 14680080 | tf_op jit(solution)/shard_map/all_gather | solution.py:22
  311.2 0.0 copy-start.1
  311.2 33.9 %convolution_multiply_fusion = f32[1792,3584]{1,0:T(8,128)} fusion(bf16[2048,1792]{1,0:T(8,128)(2,1)} %bitcast.13, bf16[2048,3584]{1,0:T(8,128)(2,1)} %all-gather.5.cloned.1.call-done), kind=kOutput, calls=%fused_computation | convolution fusion | flops 26313097216 | bytes 47710208 | tf_op jit(solution)/shard_map/dot_general | solution.py:20
  345.1 0.0 copy-done.1
Async XLA Ops:
  7.2 1.6 copy-start
  7.2 153.8 %all-gather.3.cloned.1.call-start = ((), (), s32[]{:S(2)}) async-start(), calls=%async_computation.1 | async-start | bytes 9175040 | tf_op jit(solution)/shard_map/all_gather | solution.py:18
  25.6 285.6 %all-gather.5.cloned.1.call-start = ((), (), s32[]{:S(2)}) async-start(), calls=%async_computation.2 | async-start | bytes 16515072 | tf_op jit(solution)/shard_map/all_gather | solution.py:22
  311.2 33.9 %copy-start.1 = (bf16[256,4096]{1,0:T(8,128)(2,1)S(1)}, bf16[256,4096]{1,0:T(8,128)(2,1)}, u32[]{:S(2)}) copy-start(bf16[256,4096]{1,0:T(8,128)(2,1)} %param.4) | copy-start | bytes 6291460
Sparse Core Ops, SparseCore 0:
  25.7 135.1 all-gather.2
  163.4 147.7 all-gather.4
where the time goes:
time: 352 us
  waiting for transfers between devices  147 us (42%)
  blocking collectives  135 us (38%)
  matrix products  50.7 us (14%)
  between operations  14.1 us (4%)
  local copies, waits for them, and re-layouts  5.11 us (1%)
    all_to_all x1, blocking collectives, local(): lax.all_to_all(all_columns_grad, 'dp', split_axis=1, concat_axis=0, tiled...  135 us
    all_gather x1, waiting for transfers between devices, local(): all_columns_grad = lax.all_gather(grad_gate, 'tensor', axis=1, tiled=True)  135 us
    dot_general x1, matrix products, local(): lax.dot_general(row_block, lax.all_gather(grad_gate, 'dp', axis=0, tiled=...  33.9 us
    dot_general x1, matrix products, local(): lax.dot_general(grad_out, down_weight, (((1,), (1,)), ((), ())), preferre...  16.8 us
    all_gather x1, waiting for transfers between devices, local(): lax.all_gather(grad_gate, 'dp', axis=0, tiled=True)  11.4 us
  transfers between devices with their start and end apart: 2, of which 2 were waited for; matrix products, arithmetic and copies ran while one was open for 1% of the time, Pallas kernels for 0%

commit v1 on v0

--- a/solution.py
+++ b/solution.py
@@ -15,7 +15,14 @@
     grad_up = (hidden_grad * gate_value * sigmoid_gate).astype(jnp.bfloat16)
     replicas = lax.axis_size("dp")
     token_total = grad_gate.shape[0] * replicas
-    all_columns_grad = lax.all_gather(grad_gate, "tensor", axis=1, tiled=True)
+    ring = [grad_gate]
+    for hop in range(3):
+        ring.append(lax.ppermute(ring[-1], "tensor", [(dev, (dev + 1) % 4) for dev in range(4)]))
+    all_columns_grad = jnp.roll(
+        jnp.concatenate(ring[::-1], axis=1),
+        (lax.axis_index("tensor") + 1) * ring[0].shape[1],
+        axis=1,
+    )
     row_block = lax.all_to_all(all_columns_grad, "dp", split_axis=1, concat_axis=0, tiled=True)
     factor_tile = lax.dot_general(
         row_block,

time: 352 us -> 334 us (0.949)
  blocking collectives: 135 us -> 88.3 us
  local copies, waits for them, and re-layouts: 5.11 us -> 48.7 us
  waiting for transfers between devices: 147 us -> 128 us
    all_gather x1 -> x0, waiting for transfers between devices: 135 us -> none  [local(): all_columns_grad = lax.all_gather(grad_gate, 'tensor', axis=1, tiled=True)]
    ppermute x0 -> x3, waiting for transfers between devices: none -> 128 us  [local(): lax.ppermute(ring[-1], 'tensor', [(dev, (dev + 1) % 4) for dev in range(4)])]
    all_to_all x1, blocking collectives: 135 us -> 88.3 us  [local(): lax.all_to_all(all_columns_grad, 'dp', split_axis=1, concat_axis=0, tiled...]
    dynamic_slice x0 -> x2, local copies, waits for them, and re-layouts: none -> 19.1 us  [local(): jnp.roll(jnp.concatenate(ring[::-1], axis=1), (lax.axis_index('tensor') +...]
    unnamed x4 -> x17, local copies, waits for them, and re-layouts: 1.55 us -> 18.2 us
    all_gather x1, waiting for transfers between devices: 11.4 us -> 0.01 us  [local(): lax.all_gather(grad_gate, 'dp', axis=0, tiled=True)]
    all_to_all x1, local copies, waits for them, and re-layouts: 3.56 us -> 10.1 us  [local(): lax.all_to_all(all_columns_grad, 'dp', split_axis=1, concat_axis=0, tiled...]
  transfers between devices with their start and end apart: 2 -> 4, of which waited for: 2 -> 3; matrix products, arithmetic and copies ran while one was open for 1% -> 14% of each run, Pallas kernels for 0% -> 0%
where the time goes in v1:
time: 334 us; the launch traced here: 333 us
  waiting for transfers between devices  128 us (38%)
  blocking collectives  88.3 us (26%)
  matrix products  50.7 us (15%)
  local copies, waits for them, and re-layouts  48.7 us (15%)
  between operations  14 us (4%)
    ppermute x3, waiting for transfers between devices, local(): lax.ppermute(ring[-1], 'tensor', [(dev, (dev + 1) % 4) for dev in range(4)])  128 us
    all_to_all x1, blocking collectives, local(): lax.all_to_all(all_columns_grad, 'dp', split_axis=1, concat_axis=0, tiled...  88.3 us
    dot_general x1, matrix products, local(): lax.dot_general(row_block, lax.all_gather(grad_gate, 'dp', axis=0, tiled=...  33.9 us
    dynamic_slice x2, local copies, waits for them, and re-layouts, local(): jnp.roll(jnp.concatenate(ring[::-1], axis=1), (lax.axis_index('tensor') +...  19.1 us
    unnamed x17, local copies, waits for them, and re-layouts  18.2 us
    dot_general x1, matrix products, local(): lax.dot_general(grad_out, down_weight, (((1,), (1,)), ((), ())), preferre...  16.9 us
    all_to_all x1, local copies, waits for them, and re-layouts, local(): lax.all_to_all(all_columns_grad, 'dp', split_axis=1, concat_axis=0, tiled...  10.1 us
  transfers between devices with their start and end apart: 4, of which 3 were waited for; matrix products, arithmetic and copies ran while one was open for 14% of the time, Pallas kernels for 0%

profile of v1, /device:TPU:0, one launch (start us, length us, event | category | flops | bytes accessed | tf_op | source)
XLA Modules:
  0.0 332.7 jit_solution(17324642808825691218)
XLA Ops:
  7.2 0.0 copy-start
  7.2 0.0 all-gather.2.cloned.1.call-start
  7.2 1.5 copy-done
  8.8 16.9 %fusion.8 = (bf16[256,3584]{1,0:T(8,128)(2,1)}, bf16[256,3584]{1,0:T(8,128)(2,1)}) fusion(bf16[256,3584]{1,0:T(8,128)(2,1)} %param.6, bf16[256,3584]{1,0:T(8,128)(2,1)} %param.7, bf16[256,4096]{1,0:T(8,128)(2,1)S(1)} %copy-done, bf16[3584,4096]{1,0:T(8,128)(2,1)} %param.5), kind=kOutput, calls=%fused_computation.12 | convolution fusion | flops 7529955328 | bytes 38797312 | tf_op jit(solution)/shard_map/dot_general | solution.py:8
  25.6 0.0 copy-start.2
  25.6 0.0 all-gather.2.cloned.1.call-update
  25.7 3.1 collective-permute-start
  28.8 42.2 %collective-permute-done = bf16[256,3584]{1,0:T(8,128)(2,1)S(1)} collective-permute-done((bf16[256,3584]{1,0:T(8,128)(2,1)}, bf16[256,3584]{1,0:T(8,128)(2,1)S(1)}, u32[]{:S(2)}, u32[]{:S(2)}) %collective-permute-start) | collective-permute-done | bytes 1835040 | tf_op jit(solution)/shard_map/ppermute | solution.py:20
  71.0 0.0 copy-start.3
  71.0 1.2 copy-done.3
  72.3 0.0 collective-permute-start.1
  72.3 43.1 %collective-permute-done.1 = bf16[256,3584]{1,0:T(8,128)(2,1)} collective-permute-done((bf16[256,3584]{1,0:T(8,128)(2,1)S(1)}, bf16[256,3584]{1,0:T(8,128)(2,1)}, u32[]{:S(2)}, u32[]{:S(2)}) %collective-permute-start.1) | collective-permute-done | bytes 1835040 | tf_op jit(solution)/shard_map/ppermute | solution.py:20
  115.3 0.0 collective-permute-start.2
  115.3 0.0 copy-start.4
  115.3 42.4 %collective-permute-done.2 = bf16[256,3584]{1,0:T(8,128)(2,1)} collective-permute-done((bf16[256,3584]{1,0:T(8,128)(2,1)}, bf16[256,3584]{1,0:T(8,128)(2,1)}, u32[]{:S(2)}, u32[]{:S(2)}) %collective-permute-start.2) | collective-permute-done | bytes 1835040 | tf_op jit(solution)/shard_map/ppermute | solution.py:20
  157.8 2.8 constant_dynamic-update-slice_fusion.7
  160.6 2.8 constant_dynamic-update-slice_fusion.6
  163.5 0.0 copy-done.4
  163.5 1.3 constant_dynamic-update-slice_fusion.5
  164.8 0.0 copy-done.2
  164.8 1.3 constant_dynamic-update-slice_fusion.4
  166.2 2.8 constant_dynamic-update-slice_fusion.3
  169.0 2.8 constant_dynamic-update-slice_fusion.2
  171.8 1.3 constant_dynamic-update-slice_fusion.1
  173.2 1.3 constant_dynamic-update-slice_fusion
  174.5 8.7 %constant_dynamic-slice_fusion = bf16[256,14336]{1,0:T(8,128)(2,1)} fusion(bf16[256,28672]{1,0:T(8,128)(2,1)} %constant_dynamic-update-slice_fusion, s32[]{:T(128)S(6)} %select_n.14), kind=kLoop, calls=%fused_computation.21 | loop fusion | bytes 14680068 | tf_op jit(solution)/shard_map/jit(_roll_dynamic)/dynamic_slice | solution.py:21
  183.2 10.4 %copy.6 = bf16[256,14336]{0,1:T(8,128)(2,1)} copy(bf16[256,14336]{1,0:T(8,128)(2,1)} %constant_dynamic-slice_fusion) | data formatting | bytes 14680064 | tf_op jit(solution)/shard_map/jit(_roll_dynamic)/dynamic_slice | solution.py:21
  193.6 88.3 %all_to_all.19 = bf16[256,8,1792]{0,2,1:T(8,128)(2,1)} all-to-all(bf16[256,8,1792]{0,2,1:T(8,128)(2,1)} %bitcast.7), channel_id=1, replica_groups=mesh['dp'=8,'tensor'=4] {'dp'}, dimensions={1} | all-to-all | bytes 14680064 | tf_op jit(solution)/shard_map/all_to_all | solution.py:26
  282.0 10.1 %copy.7 = bf16[8,256,1792]{2,1,0:T(8,128)(2,1)} copy(bf16[8,256,1792]{1,2,0:T(8,128)(2,1)} %bitcast.8) | data formatting | bytes 14680064 | tf_op jit(solution)/shard_map/all_to_all | solution.py:26
  292.0 0.0 all-gather.2.cloned.1.call-done
  292.0 0.0 copy-start.1
  292.0 33.9 %convolution_multiply_fusion = f32[1792,3584]{1,0:T(8,128)} fusion(bf16[2048,1792]{1,0:T(8,128)(2,1)} %bitcast.9, bf16[2048,3584]{1,0:T(8,128)(2,1)} %all-gather.2.cloned.1.call-done), kind=kOutput, calls=%fused_computation | convolution fusion | flops 26313097216 | bytes 47710208 | tf_op jit(solution)/shard_map/dot_general | solution.py:27
  325.9 0.0 copy-done.1
Async XLA Ops:
  7.2 1.6 copy-start
  7.2 284.9 %all-gather.2.cloned.1.call-start = ((), (), s32[]{:S(2)}) async-start(), calls=%async_computation.1 | async-start | bytes 16515072 | tf_op jit(solution)/shard_map/all_gather | solution.py:29
  25.6 139.2 %copy-start.2 = (bf16[256,3584]{1,0:T(8,128)(2,1)S(1)}, bf16[256,3584]{1,0:T(8,128)(2,1)}, u32[]{:S(2)}) copy-start(bf16[256,3584]{1,0:T(8,128)(2,1)} %get-tuple-element.3) | copy-start | bytes 5505028
  25.7 45.3 %collective-permute-start = (bf16[256,3584]{1,0:T(8,128)(2,1)}, bf16[256,3584]{1,0:T(8,128)(2,1)S(1)}, u32[]{:S(2)}, u32[]{:S(2)}) collective-permute-start(bf16[256,3584]{1,0:T(8,128)(2,1)} %get-tuple-element.3), channel_id=1, source_target_pairs={{0,1},{1,2},{2,3},{3,0},{4,5},{5,6},{6,7},{7,4},{8,9},{9,10},{10,1... | collective-permute-start | bytes 5505032 | tf_op jit(solution)/shard_map/ppermute | solution.py:20
  71.0 1.2 copy-start.3
  72.3 43.1 %collective-permute-start.1 = (bf16[256,3584]{1,0:T(8,128)(2,1)S(1)}, bf16[256,3584]{1,0:T(8,128)(2,1)}, u32[]{:S(2)}, u32[]{:S(2)}) collective-permute-start(bf16[256,3584]{1,0:T(8,128)(2,1)S(1)} %collective-permute-done), channel_id=1, source_target_pairs={{0,1},{1,2},{2,3},{3,0},{4,5},{5,6},{6,7},{7,4},{8,9},{9,10},{10,1... | collective-permute-start | bytes 5505032 | tf_op jit(solution)/shard_map/ppermute | solution.py:20
  115.3 42.4 %collective-permute-start.2 = (bf16[256,3584]{1,0:T(8,128)(2,1)}, bf16[256,3584]{1,0:T(8,128)(2,1)}, u32[]{:S(2)}, u32[]{:S(2)}) collective-permute-start(bf16[256,3584]{1,0:T(8,128)(2,1)} %collective-permute-done.1), channel_id=1, source_target_pairs={{0,1},{1,2},{2,3},{3,0},{4,5},{5,6},{6,7},{7,4},{8,9},{9,10},{10,1... | collective-permute-start | bytes 5505032 | tf_op jit(solution)/shard_map/ppermute | solution.py:20
  115.3 48.1 %copy-start.4 = (bf16[256,3584]{1,0:T(8,128)(2,1)S(1)}, bf16[256,3584]{1,0:T(8,128)(2,1)}, u32[]{:S(2)}) copy-start(bf16[256,3584]{1,0:T(8,128)(2,1)} %copy-done.3) | copy-start | bytes 5505028
  292.0 33.9 %copy-start.1 = (bf16[256,4096]{1,0:T(8,128)(2,1)S(1)}, bf16[256,4096]{1,0:T(8,128)(2,1)}, u32[]{:S(2)}) copy-start(bf16[256,4096]{1,0:T(8,128)(2,1)} %param.4) | copy-start | bytes 6291460
Sparse Core Ops, SparseCore 0:
  25.8 83.5 all-gather.1
